TPU v7x, 32 devices: a whole 2x2x4 slice. The times are simulated.
32 devices in a mesh: dp: 8 (over z, y), neg: 4 (over x, core).
Axes of the slice: x: 2, y: 2, z: 4, core: 2. Of those that a mesh axis runs over, the one named last changes fastest.
Arguments:
- user_embed: bfloat16 [24576, 256], P(('dp', 'neg')), may hold values from -25 to 25
- positive_embed: bfloat16 [24576, 256], P(('dp', 'neg')), may hold values from -6 to 6
- positive_ids: int32 [24576], P(('dp', 'neg')), may hold values from 0 to 1048575
- token_weights: int32 [24576], P(('dp', 'neg')), may hold values from 1 to 5
- offsets: int32 [8, 25], P('dp'), may hold values from 0 to 3072, as said below
- negative_embed: bfloat16 [32768, 256], P('neg'), may hold values from -6 to 6
- negative_ids: int32 [32768], P('neg'), may hold values from 0 to 1048575
Outputs:
- token_loss: float32 [24576], P(('dp', 'neg'))
- mean_loss: float32 [], replicated
Inputs may be any that keep to these rules, and one draw needn't show every extreme that they name: `offsets`: each row starts at 0 and does not fall; every user holds 2 or more slots; in every draw some group fills all 3072 slots.
All inputs are finite; a program needn't handle non-finite values.
Results may differ from a plain program's by a relative error of at most 0.0003.
Values may be sent and summed in bfloat16 or wider, within the bound.
No kernel may reach another device: no remote copies, remote signals or barrier semaphores. Data moves between devices by JAX's collectives and lax.ppermute only.
A program may use at most 64 MiB of HBM per device.

v0:
```python
import math
import jax
import jax.numpy as jnp
from jax import lax
from jax.sharding import PartitionSpec as P

floor_value = -1e30


def merged(value, axis, join):
    pieces = jax.tree.map(lambda part: lax.all_gather(part, axis), value)
    head = jax.tree.map(lambda part: part[0], pieces)
    tail = jax.tree.map(lambda part: part[1:], pieces)
    total, _ = lax.scan(lambda total, share: (join(total, share), None), head, tail)
    return total


def shard_partials(rows, row_ids, columns, column_ids, scale):
    logits = (
        lax.dot_general(rows, columns, (((1,), (1,)), ((), ())), preferred_element_type=jnp.float32)
        * scale
    )
    hit = row_ids[:, None] == column_ids[None, :]
    peak = jnp.max(jnp.where(hit, floor_value, logits), axis=1)
    summed = jnp.sum(jnp.where(hit, 0.0, jnp.exp(logits - peak[:, None])), axis=1)
    return (peak, summed)


def combine(first, second):
    peak = jnp.maximum(first[0], second[0])
    return (peak, first[1] * jnp.exp(first[0] - peak) + second[1] * jnp.exp(second[0] - peak))


def shards(
    user_embed, positive_embed, positive_ids, token_weights, offsets, negative_embed, negative_ids
):
    tok_rows = user_embed.shape[0]
    width = user_embed.shape[1]
    scale = 3.0 / math.sqrt(width)
    positions = lax.axis_index("neg") * tok_rows + jnp.arange(tok_rows, dtype=jnp.int32)
    ends = offsets[0, 1:]
    last_slot = jnp.any(positions[:, None] + 1 == ends[None, :], axis=1)
    live = (positions < offsets[0, -1]) & jnp.logical_not(last_slot)
    weight = token_weights.astype(jnp.float32)
    live_weight = weight * live.astype(jnp.float32)
    rows = lax.all_gather(user_embed, "neg", axis=0, tiled=True)
    row_ids = lax.all_gather(positive_ids, "neg", axis=0, tiled=True)
    number = rows.shape[0]
    block = math.gcd(number, 512)
    blocks = rows.reshape(number // block, block, width)
    id_blocks = row_ids.reshape(number // block, block)

    def one_block(pair):
        return shard_partials(pair[0], pair[1], negative_embed, negative_ids, scale)

    peaks, sums = lax.map(one_block, (blocks, id_blocks))
    new_peaks = peaks.reshape(number)
    new_sums = sums.reshape(number)
    peaks = new_peaks
    sums = new_sums
    peaks, sums = merged((peaks, sums), "neg", combine)
    own_start = lax.axis_index("neg") * tok_rows
    peaks = lax.dynamic_slice_in_dim(peaks, own_start, tok_rows, 0)
    sums = lax.dynamic_slice_in_dim(sums, own_start, tok_rows, 0)
    positive = (
        jnp.sum(user_embed.astype(jnp.float32) * positive_embed.astype(jnp.float32), axis=1) * scale
    )
    top = jnp.maximum(peaks, positive)
    lse = top + jnp.log(sums * jnp.exp(peaks - top) + jnp.exp(positive - top))
    token_loss = jnp.where(live, lse - positive, 0.0).astype(jnp.float32)
    weighted = jnp.sum(weight * token_loss)
    total, count = lax.psum((weighted, jnp.sum(live_weight)), ("dp", "neg"))
    return (token_loss, total / count)


def solution(mesh):
    in_specs = (
        P(("dp", "neg"), None),
        P(("dp", "neg"), None),
        P(("dp", "neg")),
        P(("dp", "neg")),
        P("dp", None),
        P("neg", None),
        P("neg"),
    )
    out_specs = (P(("dp", "neg")), P())
    return jax.shard_map(shards, mesh=mesh, in_specs=in_specs, out_specs=out_specs, check_vma=False)
```

profile of v0, /device:TPU:0, one launch (start us, length us, event | category | flops | bytes accessed | tf_op | source)
XLA Modules:
  0.0 153.4 jit_solution(13548246562837746475)
XLA Ops:
  7.2 0.7 all-gather.5.cloned.1.call-update
  7.9 0.7 reshape.22
  8.6 6.2 %all-gather = s32[4,1,768]{2,1,0:T(1,128)S(1)} all-gather(s32[1,1,768]{2,1,0:T(1,128)S(1)} %reshape.22), channel_id=1, replica_groups=mesh['dp'=8,'neg'=4] {'neg'}, dimensions={0}, use_global_device_ids=true | all-gather | bytes 15360 | tf_op jit(solution)/shard_map/all_gather | solution.py:47
  14.9 1.2 slice.18
  16.1 0.7 slice_bitcast_fusion
  16.9 1.3 multiply_reduce_fusion
  18.2 13.7 %all-gather.5.cloned.1.call-done = bf16[3072,256]{1,0:T(8,128)(2,1)} async-done(((bf16[768,256]{1,0:T(8,128)(2,1)}), bf16[3072,256]{1,0:T(8,128)(2,1)}) %all-gather.5.cloned.1.call-update) | async-done | bytes 1572880 | tf_op jit(solution)/shard_map/all_gather | solution.py:46
  31.9 59.9 %while.24 = (s32[]{:T(128)}, f32[6,512]{1,0:T(8,128)S(1)}, f32[6,512]{1,0:T(8,128)S(1)}, s32[6,512]{1,0:T(8,128)S(1)}, s32[8192]{0:T(1024)}, /*index=5*/bf16[6,5...) while((s32[]{:T(128)}, f32[6,512]{1,0:T(8,128)S(1)}, f32[6,512]{1,0:T(8,128)S(1)}, ...), condition=%wide.region_4.5_spmd, body=%wide.region_1.4_spmd.sunk | while | flops 2185231360 | bytes 38230660 | solution.py:56
  31.9 5.1 %fusion.16 = (f32[512]{0:T(512)S(1)}, f32[512,8192]{1,0:T(8,128)S(1)}) fusion(s32[8192]{0:T(1024)} %get-tuple-element.215, s32[512]{0:T(512)S(1)} %bitcast.44, bf16[8192,256]{1,0:T(8,128)(2,1)} %get-tuple-element.217, bf16[6,512,256]{2,1,0:T(8,128)(2,1)} %get-tuple-element.216, s32[]{:T(128)} %get-tuple-element.202), kind=kOutput, calls=%fused_computation.2.clone.1 | convolution fusion | flops 2164260352 | bytes 21271040 | tf_op jit(solution)/shard_map/while/body/eval_jaxpr/dot_general | solution.py:20
  37.1 4.6 %fusion.17 = f32[512]{0:T(512)S(1)} fusion(f32[512,8192]{1,0:T(8,128)S(1)} %get-tuple-element.183, f32[512]{0:T(512)S(1)} %get-tuple-element.182, s32[8192]{0:T(1024)S(1)} %copy-done, s32[512]{0:T(512)S(1)} %bitcast.45), kind=kLoop, calls=%fused_computation.3.clone.1 | loop fusion | flops 20971008 | bytes 16816128 | tf_op jit(solution)/shard_map/while/body/eval_jaxpr/reduce_sum | solution.py:25
  41.9 5.1 %fusion.16 = (f32[512]{0:T(512)S(1)}, f32[512,8192]{1,0:T(8,128)S(1)}) fusion(s32[8192]{0:T(1024)} %get-tuple-element.215, s32[512]{0:T(512)S(1)} %bitcast.44, bf16[8192,256]{1,0:T(8,128)(2,1)} %get-tuple-element.217, bf16[6,512,256]{2,1,0:T(8,128)(2,1)} %get-tuple-element.216, s32[]{:T(128)} %get-tuple-element.202), kind=kOutput, calls=%fused_computation.2.clone.1 | convolution fusion | flops 2164260352 | bytes 21271040 | tf_op jit(solution)/shard_map/while/body/eval_jaxpr/dot_general | solution.py:20
  47.1 4.6 %fusion.17 = f32[512]{0:T(512)S(1)} fusion(f32[512,8192]{1,0:T(8,128)S(1)} %get-tuple-element.183, f32[512]{0:T(512)S(1)} %get-tuple-element.182, s32[8192]{0:T(1024)S(1)} %copy-done, s32[512]{0:T(512)S(1)} %bitcast.45), kind=kLoop, calls=%fused_computation.3.clone.1 | loop fusion | flops 20971008 | bytes 16816128 | tf_op jit(solution)/shard_map/while/body/eval_jaxpr/reduce_sum | solution.py:25
  51.9 5.1 %fusion.16 = (f32[512]{0:T(512)S(1)}, f32[512,8192]{1,0:T(8,128)S(1)}) fusion(s32[8192]{0:T(1024)} %get-tuple-element.215, s32[512]{0:T(512)S(1)} %bitcast.44, bf16[8192,256]{1,0:T(8,128)(2,1)} %get-tuple-element.217, bf16[6,512,256]{2,1,0:T(8,128)(2,1)} %get-tuple-element.216, s32[]{:T(128)} %get-tuple-element.202), kind=kOutput, calls=%fused_computation.2.clone.1 | convolution fusion | flops 2164260352 | bytes 21271040 | tf_op jit(solution)/shard_map/while/body/eval_jaxpr/dot_general | solution.py:20
  57.1 4.6 %fusion.17 = f32[512]{0:T(512)S(1)} fusion(f32[512,8192]{1,0:T(8,128)S(1)} %get-tuple-element.183, f32[512]{0:T(512)S(1)} %get-tuple-element.182, s32[8192]{0:T(1024)S(1)} %copy-done, s32[512]{0:T(512)S(1)} %bitcast.45), kind=kLoop, calls=%fused_computation.3.clone.1 | loop fusion | flops 20971008 | bytes 16816128 | tf_op jit(solution)/shard_map/while/body/eval_jaxpr/reduce_sum | solution.py:25
  61.9 5.1 %fusion.16 = (f32[512]{0:T(512)S(1)}, f32[512,8192]{1,0:T(8,128)S(1)}) fusion(s32[8192]{0:T(1024)} %get-tuple-element.215, s32[512]{0:T(512)S(1)} %bitcast.44, bf16[8192,256]{1,0:T(8,128)(2,1)} %get-tuple-element.217, bf16[6,512,256]{2,1,0:T(8,128)(2,1)} %get-tuple-element.216, s32[]{:T(128)} %get-tuple-element.202), kind=kOutput, calls=%fused_computation.2.clone.1 | convolution fusion | flops 2164260352 | bytes 21271040 | tf_op jit(solution)/shard_map/while/body/eval_jaxpr/dot_general | solution.py:20
  67.1 4.6 %fusion.17 = f32[512]{0:T(512)S(1)} fusion(f32[512,8192]{1,0:T(8,128)S(1)} %get-tuple-element.183, f32[512]{0:T(512)S(1)} %get-tuple-element.182, s32[8192]{0:T(1024)S(1)} %copy-done, s32[512]{0:T(512)S(1)} %bitcast.45), kind=kLoop, calls=%fused_computation.3.clone.1 | loop fusion | flops 20971008 | bytes 16816128 | tf_op jit(solution)/shard_map/while/body/eval_jaxpr/reduce_sum | solution.py:25
  71.9 5.1 %fusion.16 = (f32[512]{0:T(512)S(1)}, f32[512,8192]{1,0:T(8,128)S(1)}) fusion(s32[8192]{0:T(1024)} %get-tuple-element.215, s32[512]{0:T(512)S(1)} %bitcast.44, bf16[8192,256]{1,0:T(8,128)(2,1)} %get-tuple-element.217, bf16[6,512,256]{2,1,0:T(8,128)(2,1)} %get-tuple-element.216, s32[]{:T(128)} %get-tuple-element.202), kind=kOutput, calls=%fused_computation.2.clone.1 | convolution fusion | flops 2164260352 | bytes 21271040 | tf_op jit(solution)/shard_map/while/body/eval_jaxpr/dot_general | solution.py:20
  77.0 4.6 %fusion.17 = f32[512]{0:T(512)S(1)} fusion(f32[512,8192]{1,0:T(8,128)S(1)} %get-tuple-element.183, f32[512]{0:T(512)S(1)} %get-tuple-element.182, s32[8192]{0:T(1024)S(1)} %copy-done, s32[512]{0:T(512)S(1)} %bitcast.45), kind=kLoop, calls=%fused_computation.3.clone.1 | loop fusion | flops 20971008 | bytes 16816128 | tf_op jit(solution)/shard_map/while/body/eval_jaxpr/reduce_sum | solution.py:25
  81.9 5.1 %fusion.16 = (f32[512]{0:T(512)S(1)}, f32[512,8192]{1,0:T(8,128)S(1)}) fusion(s32[8192]{0:T(1024)} %get-tuple-element.215, s32[512]{0:T(512)S(1)} %bitcast.44, bf16[8192,256]{1,0:T(8,128)(2,1)} %get-tuple-element.217, bf16[6,512,256]{2,1,0:T(8,128)(2,1)} %get-tuple-element.216, s32[]{:T(128)} %get-tuple-element.202), kind=kOutput, calls=%fused_computation.2.clone.1 | convolution fusion | flops 2164260352 | bytes 21271040 | tf_op jit(solution)/shard_map/while/body/eval_jaxpr/dot_general | solution.py:20
  87.0 4.6 %fusion.17 = f32[512]{0:T(512)S(1)} fusion(f32[512,8192]{1,0:T(8,128)S(1)} %get-tuple-element.183, f32[512]{0:T(512)S(1)} %get-tuple-element.182, s32[8192]{0:T(1024)S(1)} %copy-done, s32[512]{0:T(512)S(1)} %bitcast.45), kind=kLoop, calls=%fused_computation.3.clone.1 | loop fusion | flops 20971008 | bytes 16816128 | tf_op jit(solution)/shard_map/while/body/eval_jaxpr/reduce_sum | solution.py:25
  91.8 5.2 %all-gather.2 = f32[4,1,3072]{2,1,0:T(1,128)S(1)} all-gather(f32[1,1,3072]{2,1,0:T(1,128)S(1)} %reshape.26), channel_id=1, replica_groups=mesh['dp'=8,'neg'=4] {'neg'}, dimensions={0}, use_global_device_ids=true | all-gather | bytes 61440 | tf_op jit(solution)/shard_map/all_gather | solution.py:11
  97.1 5.2 %all-gather.1 = f32[4,1,3072]{2,1,0:T(1,128)S(1)} all-gather(f32[1,1,3072]{2,1,0:T(1,128)S(1)} %reshape.24), channel_id=1, replica_groups=mesh['dp'=8,'neg'=4] {'neg'}, dimensions={0}, use_global_device_ids=true | all-gather | bytes 61440 | tf_op jit(solution)/shard_map/all_gather | solution.py:11
  102.6 2.0 %select_reduce_fusion = (f32[]{:T(128)}, f32[]{:T(128)}, f32[768]{0:T(1024)}) fusion(s32[768]{0:T(1024)S(1)} %copy-done.1, pred[768]{0:T(1024)(128)(4,1)S(1)} %compare_reduce_fusion, s32[]{:T(128)} %bitcast.6, s32[]{:T(128)S(6)} %mul.31, f32[3072]{0:T(1024)S(1)} %get-tuple-element.71, s32[]{:T(128)S(6)} %select_n.15, f32[768]{0:T(1024)S(1)} %multiply_reduce_fusion, ...), kind=kLoop, calls=%fused_computation.16 | loop fusion | flops 13822 | bytes 16148 | tf_op jit(solution)/shard_map/reduce_sum | solution.py:72
  104.6 39.5 %all-reduce = (f32[]{:T(128)}, f32[]{:T(128)}) all-reduce(f32[]{:T(128)} %get-tuple-element.73, f32[]{:T(128)} %get-tuple-element.72), channel_id=1, replica_groups=mesh['dp'=8,'neg'=4] {'dp','neg'}, use_global_device_ids=true, to_apply=%region_9.10 | all-reduce | flops 2 | bytes 16 | tf_op jit(solution)/shard_map/psum | solution.py:72
  (54 shorter events, 1.4 us)
Async XLA Ops:
  7.2 24.8 %all-gather.5.cloned.1.call-start = ((), (), s32[]{:S(2)}) async-start(), calls=%async_computation | async-start | bytes 1966080 | tf_op jit(solution)/shard_map/all_gather | solution.py:46
  31.9 70.7 %copy-start.1 = (s32[768]{0:T(1024)S(1)}, s32[768]{0:T(1024)}, u32[]{:S(2)}) copy-start(s32[768]{0:T(1024)} %param.14) | copy-start | bytes 9220
  31.9 5.2 %copy-start = (s32[8192]{0:T(1024)S(1)}, s32[8192]{0:T(1024)}, u32[]{:S(2)}) copy-start(s32[8192]{0:T(1024)} %get-tuple-element.215) | copy-start | bytes 98308 | tf_op jit(solution)/shard_map/while
  41.9 5.2 %copy-start = (s32[8192]{0:T(1024)S(1)}, s32[8192]{0:T(1024)}, u32[]{:S(2)}) copy-start(s32[8192]{0:T(1024)} %get-tuple-element.215) | copy-start | bytes 98308 | tf_op jit(solution)/shard_map/while
  51.9 5.2 %copy-start = (s32[8192]{0:T(1024)S(1)}, s32[8192]{0:T(1024)}, u32[]{:S(2)}) copy-start(s32[8192]{0:T(1024)} %get-tuple-element.215) | copy-start | bytes 98308 | tf_op jit(solution)/shard_map/while
  61.9 5.2 %copy-start = (s32[8192]{0:T(1024)S(1)}, s32[8192]{0:T(1024)}, u32[]{:S(2)}) copy-start(s32[8192]{0:T(1024)} %get-tuple-element.215) | copy-start | bytes 98308 | tf_op jit(solution)/shard_map/while
  71.9 5.2 %copy-start = (s32[8192]{0:T(1024)S(1)}, s32[8192]{0:T(1024)}, u32[]{:S(2)}) copy-start(s32[8192]{0:T(1024)} %get-tuple-element.215) | copy-start | bytes 98308 | tf_op jit(solution)/shard_map/while
  81.8 5.2 %copy-start = (s32[8192]{0:T(1024)S(1)}, s32[8192]{0:T(1024)}, u32[]{:S(2)}) copy-start(s32[8192]{0:T(1024)} %get-tuple-element.215) | copy-start | bytes 98308 | tf_op jit(solution)/shard_map/while
Sparse Core Ops, SparseCore 0:
  9.5 22.3 all-gather.4
where the time goes:
time: 154 us; the launch traced here: 153 us
  blocking collectives  56.2 us (36%)
  other arithmetic  31.4 us (20%)
  matrix products  30.9 us (20%)
  between operations  16.6 us (11%)
  waiting for transfers between devices  14.4 us (9%)
  local copies, waits for them, and re-layouts  3.64 us (2%)
    psum x1, blocking collectives, shards(): total, count = lax.psum((weighted, jnp.sum(live_weight)), ('dp', 'neg'))  39.5 us
    dot_general x6, matrix products, shard_partials(): lax.dot_general(rows, columns, (((1,), (1,)), ((), ())), preferred_elemen...  30.9 us
    reduce_sum x6, other arithmetic, shard_partials(): jnp.sum(jnp.where(hit, 0.0, jnp.exp(logits - peak[:, None])), axis=1)  27.9 us
    all_gather x1, waiting for transfers between devices, shards(): rows = lax.all_gather(user_embed, 'neg', axis=0, tiled=True)  13.7 us
    all_gather x2, blocking collectives, merged(): pieces = jax.tree.map(lambda part: lax.all_gather(part, axis), value)  10.4 us
    all_gather x1, blocking collectives, shards(): row_ids = lax.all_gather(positive_ids, 'neg', axis=0, tiled=True)  6.2 us
  transfers between devices with their start and end apart: 1, of which 1 were waited for; matrix products, arithmetic and copies ran while one was open for 3% of the time, Pallas kernels for 0%

commit v1 on v0

--- a/solution.py
+++ b/solution.py
@@ -5,6 +5,19 @@
 from jax.sharding import PartitionSpec as P
 
 floor_value = -1e30
+
+
+def recast_the_sums_all(matrix, net_axis):
+    devs = lax.axis_size(net_axis)
+    gallery = tuple(((m, (m + 1) % devs) for m in range(devs)))
+
+    def expand_row(even):
+        if len(even) == devs:
+            return even
+        return expand_row([lax.ppermute(even[0], perm=gallery, axis_name=net_axis), *even])
+
+    val2 = jnp.concatenate(expand_row([matrix]), 0)
+    return jnp.roll(val2, (lax.axis_index(net_axis) + 1) * matrix.shape[0], 0)
 
 
 def merged(value, axis, join):
@@ -43,7 +56,7 @@
     live = (positions < offsets[0, -1]) & jnp.logical_not(last_slot)
     weight = token_weights.astype(jnp.float32)
     live_weight = weight * live.astype(jnp.float32)
-    rows = lax.all_gather(user_embed, "neg", axis=0, tiled=True)
+    rows = recast_the_sums_all(user_embed, "neg")
     row_ids = lax.all_gather(positive_ids, "neg", axis=0, tiled=True)
     number = rows.shape[0]
     block = math.gcd(number, 512)

time: 154 us -> 140 us (0.909)
  between operations: 16.6 us -> 3.25 us
  matrix products: 30.9 us -> 29.3 us
    ppermute x0 -> x3, waiting for transfers between devices: none -> 14.8 us  [expand_row(): lax.ppermute(even[0], perm=gallery, axis_name=net_axis)]
    all_gather x1 -> x0, waiting for transfers between devices: 13.7 us -> none  [shards(): rows = lax.all_gather(user_embed, 'neg', axis=0, tiled=True)]
    dot_general x6, matrix products: 30.9 us -> 29.3 us  [shard_partials(): lax.dot_general(rows, columns, (((1,), (1,)), ((), ())), preferred_elemen...]
  transfers between devices with their start and end apart: 1 -> 3, of which waited for: 1 -> 2; matrix products, arithmetic and copies ran while one was open for 3% -> 3% of each run, Pallas kernels for 0% -> 0%
where the time goes in v1:
time: 140 us
  blocking collectives  57.3 us (41%)
  other arithmetic  30 us (21%)
  matrix products  29.3 us (21%)
  waiting for transfers between devices  14.8 us (11%)
  local copies, waits for them, and re-layouts  4.43 us (3%)
  between operations  3.25 us (2%)
    psum x1, blocking collectives, shards(): total, count = lax.psum((weighted, jnp.sum(live_weight)), ('dp', 'neg'))  40.6 us
    dot_general x6, matrix products, shard_partials(): lax.dot_general(rows, columns, (((1,), (1,)), ((), ())), preferred_elemen...  29.3 us
    reduce_sum x6, other arithmetic, shard_partials(): jnp.sum(jnp.where(hit, 0.0, jnp.exp(logits - peak[:, None])), axis=1)  26.5 us
    ppermute x3, waiting for transfers between devices, expand_row(): lax.ppermute(even[0], perm=gallery, axis_name=net_axis)  14.8 us
    all_gather x2, blocking collectives, merged(): pieces = jax.tree.map(lambda part: lax.all_gather(part, axis), value)  10.4 us
    all_gather x1, blocking collectives, shards(): row_ids = lax.all_gather(positive_ids, 'neg', axis=0, tiled=True)  6.25 us
  transfers between devices with their start and end apart: 3, of which 2 were waited for; matrix products, arithmetic and copies ran while one was open for 3% of the time, Pallas kernels for 0%

profile of v1, /device:TPU:0, one launch (start us, length us, event | category | flops | bytes accessed | tf_op | source)
XLA Modules:
  0.0 140.0 jit_solution(13950672036128355245)
XLA Ops:
  1.2 7.6 %collective-permute-done = bf16[768,256]{1,0:T(8,128)(2,1)S(1)} collective-permute-done((bf16[768,256]{1,0:T(8,128)(2,1)}, bf16[768,256]{1,0:T(8,128)(2,1)S(1)}, u32[]{:S(2)}, u32[]{:S(2)}) %collective-permute-start) | collective-permute-done | bytes 393248 | tf_op jit(solution)/shard_map/ppermute | solution.py:17
  8.8 7.2 %collective-permute-done.1 = bf16[768,256]{1,0:T(8,128)(2,1)S(1)} collective-permute-done((bf16[768,256]{1,0:T(8,128)(2,1)S(1)}, bf16[768,256]{1,0:T(8,128)(2,1)S(1)}, u32[]{:S(2)}, u32[]{:S(2)}) %collective-permute-start.1) | collective-permute-done | bytes 393248 | tf_op jit(solution)/shard_map/ppermute | solution.py:17
  16.0 0.7 slice_bitcast_fusion
  16.7 1.2 slice.18
  18.0 0.7 reshape.22
  18.6 6.3 %all-gather = s32[4,1,768]{2,1,0:T(1,128)S(1)} all-gather(s32[1,1,768]{2,1,0:T(1,128)S(1)} %reshape.22), channel_id=1, replica_groups=mesh['dp'=8,'neg'=4] {'neg'}, dimensions={0}, use_global_device_ids=true | all-gather | bytes 15360 | tf_op jit(solution)/shard_map/all_gather | solution.py:60
  25.1 1.3 multiply_reduce_fusion
  27.3 56.9 %while.24 = (s32[]{:T(128)}, f32[6,512]{1,0:T(8,128)S(1)}, f32[6,512]{1,0:T(8,128)S(1)}, s32[6,512]{1,0:T(8,128)S(1)}, s32[8192]{0:T(1024)S(1)}, /*index=5*/bf16...) while((s32[]{:T(128)}, f32[6,512]{1,0:T(8,128)S(1)}, f32[6,512]{1,0:T(8,128)S(1)}, ...), condition=%wide.region_4.5_spmd, body=%wide.region_1.4_spmd.sunk | while | flops 2185231360 | bytes 38099052 | solution.py:69
  27.3 4.9 %fusion.16 = (f32[512]{0:T(512)S(1)}, f32[512,8192]{1,0:T(8,128)S(1)}) fusion(s32[8192]{0:T(1024)S(1)} %get-tuple-element.215, s32[512]{0:T(512)S(1)} %bitcast.45, bf16[8192,256]{1,0:T(8,128)(2,1)} %get-tuple-element.217, bf16[6,512,256]{2,1,0:T(8,128)(2,1)S(1)} %get-tuple-element.216, s32[]{:T(128)} %get-tuple-element.202), kind=kOutput, calls=%fused_computation.2.clone.1 | convolution fusion | flops 2164260352 | bytes 21270532 | tf_op jit(solution)/shard_map/while/body/eval_jaxpr/dot_general | solution.py:33
  32.2 4.4 %fusion.17 = f32[512]{0:T(512)S(1)} fusion(f32[512,8192]{1,0:T(8,128)S(1)} %get-tuple-element.183, f32[512]{0:T(512)S(1)} %get-tuple-element.182, s32[8192]{0:T(1024)S(1)} %get-tuple-element.215, s32[512]{0:T(512)S(1)} %bitcast.46), kind=kLoop, calls=%fused_computation.3.clone.1 | loop fusion | flops 20971008 | bytes 16816128 | tf_op jit(solution)/shard_map/while/body/eval_jaxpr/reduce_sum | solution.py:38
  36.8 4.9 %fusion.16 = (f32[512]{0:T(512)S(1)}, f32[512,8192]{1,0:T(8,128)S(1)}) fusion(s32[8192]{0:T(1024)S(1)} %get-tuple-element.215, s32[512]{0:T(512)S(1)} %bitcast.45, bf16[8192,256]{1,0:T(8,128)(2,1)} %get-tuple-element.217, bf16[6,512,256]{2,1,0:T(8,128)(2,1)S(1)} %get-tuple-element.216, s32[]{:T(128)} %get-tuple-element.202), kind=kOutput, calls=%fused_computation.2.clone.1 | convolution fusion | flops 2164260352 | bytes 21270532 | tf_op jit(solution)/shard_map/while/body/eval_jaxpr/dot_general | solution.py:33
  41.7 4.4 %fusion.17 = f32[512]{0:T(512)S(1)} fusion(f32[512,8192]{1,0:T(8,128)S(1)} %get-tuple-element.183, f32[512]{0:T(512)S(1)} %get-tuple-element.182, s32[8192]{0:T(1024)S(1)} %get-tuple-element.215, s32[512]{0:T(512)S(1)} %bitcast.46), kind=kLoop, calls=%fused_computation.3.clone.1 | loop fusion | flops 20971008 | bytes 16816128 | tf_op jit(solution)/shard_map/while/body/eval_jaxpr/reduce_sum | solution.py:38
  46.3 4.9 %fusion.16 = (f32[512]{0:T(512)S(1)}, f32[512,8192]{1,0:T(8,128)S(1)}) fusion(s32[8192]{0:T(1024)S(1)} %get-tuple-element.215, s32[512]{0:T(512)S(1)} %bitcast.45, bf16[8192,256]{1,0:T(8,128)(2,1)} %get-tuple-element.217, bf16[6,512,256]{2,1,0:T(8,128)(2,1)S(1)} %get-tuple-element.216, s32[]{:T(128)} %get-tuple-element.202), kind=kOutput, calls=%fused_computation.2.clone.1 | convolution fusion | flops 2164260352 | bytes 21270532 | tf_op jit(solution)/shard_map/while/body/eval_jaxpr/dot_general | solution.py:33
  51.1 4.4 %fusion.17 = f32[512]{0:T(512)S(1)} fusion(f32[512,8192]{1,0:T(8,128)S(1)} %get-tuple-element.183, f32[512]{0:T(512)S(1)} %get-tuple-element.182, s32[8192]{0:T(1024)S(1)} %get-tuple-element.215, s32[512]{0:T(512)S(1)} %bitcast.46), kind=kLoop, calls=%fused_computation.3.clone.1 | loop fusion | flops 20971008 | bytes 16816128 | tf_op jit(solution)/shard_map/while/body/eval_jaxpr/reduce_sum | solution.py:38
  55.7 4.9 %fusion.16 = (f32[512]{0:T(512)S(1)}, f32[512,8192]{1,0:T(8,128)S(1)}) fusion(s32[8192]{0:T(1024)S(1)} %get-tuple-element.215, s32[512]{0:T(512)S(1)} %bitcast.45, bf16[8192,256]{1,0:T(8,128)(2,1)} %get-tuple-element.217, bf16[6,512,256]{2,1,0:T(8,128)(2,1)S(1)} %get-tuple-element.216, s32[]{:T(128)} %get-tuple-element.202), kind=kOutput, calls=%fused_computation.2.clone.1 | convolution fusion | flops 2164260352 | bytes 21270532 | tf_op jit(solution)/shard_map/while/body/eval_jaxpr/dot_general | solution.py:33
  60.6 4.4 %fusion.17 = f32[512]{0:T(512)S(1)} fusion(f32[512,8192]{1,0:T(8,128)S(1)} %get-tuple-element.183, f32[512]{0:T(512)S(1)} %get-tuple-element.182, s32[8192]{0:T(1024)S(1)} %get-tuple-element.215, s32[512]{0:T(512)S(1)} %bitcast.46), kind=kLoop, calls=%fused_computation.3.clone.1 | loop fusion | flops 20971008 | bytes 16816128 | tf_op jit(solution)/shard_map/while/body/eval_jaxpr/reduce_sum | solution.py:38
  65.2 4.9 %fusion.16 = (f32[512]{0:T(512)S(1)}, f32[512,8192]{1,0:T(8,128)S(1)}) fusion(s32[8192]{0:T(1024)S(1)} %get-tuple-element.215, s32[512]{0:T(512)S(1)} %bitcast.45, bf16[8192,256]{1,0:T(8,128)(2,1)} %get-tuple-element.217, bf16[6,512,256]{2,1,0:T(8,128)(2,1)S(1)} %get-tuple-element.216, s32[]{:T(128)} %get-tuple-element.202), kind=kOutput, calls=%fused_computation.2.clone.1 | convolution fusion | flops 2164260352 | bytes 21270532 | tf_op jit(solution)/shard_map/while/body/eval_jaxpr/dot_general | solution.py:33
  70.1 4.4 %fusion.17 = f32[512]{0:T(512)S(1)} fusion(f32[512,8192]{1,0:T(8,128)S(1)} %get-tuple-element.183, f32[512]{0:T(512)S(1)} %get-tuple-element.182, s32[8192]{0:T(1024)S(1)} %get-tuple-element.215, s32[512]{0:T(512)S(1)} %bitcast.46), kind=kLoop, calls=%fused_computation.3.clone.1 | loop fusion | flops 20971008 | bytes 16816128 | tf_op jit(solution)/shard_map/while/body/eval_jaxpr/reduce_sum | solution.py:38
  74.7 4.9 %fusion.16 = (f32[512]{0:T(512)S(1)}, f32[512,8192]{1,0:T(8,128)S(1)}) fusion(s32[8192]{0:T(1024)S(1)} %get-tuple-element.215, s32[512]{0:T(512)S(1)} %bitcast.45, bf16[8192,256]{1,0:T(8,128)(2,1)} %get-tuple-element.217, bf16[6,512,256]{2,1,0:T(8,128)(2,1)S(1)} %get-tuple-element.216, s32[]{:T(128)} %get-tuple-element.202), kind=kOutput, calls=%fused_computation.2.clone.1 | convolution fusion | flops 2164260352 | bytes 21270532 | tf_op jit(solution)/shard_map/while/body/eval_jaxpr/dot_general | solution.py:33
  79.6 4.4 %fusion.17 = f32[512]{0:T(512)S(1)} fusion(f32[512,8192]{1,0:T(8,128)S(1)} %get-tuple-element.183, f32[512]{0:T(512)S(1)} %get-tuple-element.182, s32[8192]{0:T(1024)S(1)} %get-tuple-element.215, s32[512]{0:T(512)S(1)} %bitcast.46), kind=kLoop, calls=%fused_computation.3.clone.1 | loop fusion | flops 20971008 | bytes 16816128 | tf_op jit(solution)/shard_map/while/body/eval_jaxpr/reduce_sum | solution.py:38
  84.2 5.2 %all-gather.2 = f32[4,1,3072]{2,1,0:T(1,128)S(1)} all-gather(f32[1,1,3072]{2,1,0:T(1,128)S(1)} %reshape.26), channel_id=1, replica_groups=mesh['dp'=8,'neg'=4] {'neg'}, dimensions={0}, use_global_device_ids=true | all-gather | bytes 61440 | tf_op jit(solution)/shard_map/all_gather | solution.py:24
  89.4 5.2 %all-gather.1 = f32[4,1,3072]{2,1,0:T(1,128)S(1)} all-gather(f32[1,1,3072]{2,1,0:T(1,128)S(1)} %reshape.24), channel_id=1, replica_groups=mesh['dp'=8,'neg'=4] {'neg'}, dimensions={0}, use_global_device_ids=true | all-gather | bytes 61440 | tf_op jit(solution)/shard_map/all_gather | solution.py:24
  94.9 2.0 %select_reduce_fusion = (f32[]{:T(128)}, f32[]{:T(128)}, f32[768]{0:T(1024)}) fusion(s32[768]{0:T(1024)S(1)} %copy-done.2, pred[768]{0:T(1024)(128)(4,1)S(1)} %compare_reduce_fusion, s32[]{:T(128)} %bitcast.6, s32[]{:T(128)S(6)} %mul.34, f32[3072]{0:T(1024)S(1)} %get-tuple-element.71, s32[]{:T(128)S(6)} %select_n.30, f32[768]{0:T(1024)S(1)} %multiply_reduce_fusion, ...), kind=kLoop, calls=%fused_computation.24 | loop fusion | flops 13822 | bytes 16148 | tf_op jit(solution)/shard_map/reduce_sum | solution.py:85
  96.9 40.6 %all-reduce = (f32[]{:T(128)}, f32[]{:T(128)}) all-reduce(f32[]{:T(128)} %get-tuple-element.73, f32[]{:T(128)} %get-tuple-element.72), channel_id=1, replica_groups=mesh['dp'=8,'neg'=4] {'dp','neg'}, use_global_device_ids=true, to_apply=%region_9.10 | all-reduce | flops 2 | bytes 16 | tf_op jit(solution)/shard_map/psum | solution.py:85
  (58 shorter events, 2.8 us)
Async XLA Ops:
  0.6 25.9 %copy-start = (bf16[768,256]{1,0:T(8,128)(2,1)S(1)}, bf16[768,256]{1,0:T(8,128)(2,1)}, u32[]{:S(2)}) copy-start(bf16[768,256]{1,0:T(8,128)(2,1)} %param.11) | copy-start | bytes 1179652
  0.6 8.1 %collective-permute-start = (bf16[768,256]{1,0:T(8,128)(2,1)}, bf16[768,256]{1,0:T(8,128)(2,1)S(1)}, u32[]{:S(2)}, u32[]{:S(2)}) collective-permute-start(bf16[768,256]{1,0:T(8,128)(2,1)} %param.11), channel_id=1, source_target_pairs={{0,1},{1,2},{2,3},{3,0},{4,5},{5,6},{6,7},{7,4},{8,9},{9,10},{10,1... | collective-permute-start | bytes 1179656 | tf_op jit(solution)/shard_map/ppermute | solution.py:17
  8.8 7.2 %collective-permute-start.1 = (bf16[768,256]{1,0:T(8,128)(2,1)S(1)}, bf16[768,256]{1,0:T(8,128)(2,1)S(1)}, u32[]{:S(2)}, u32[]{:S(2)}) collective-permute-start(bf16[768,256]{1,0:T(8,128)(2,1)S(1)} %collective-permute-done), channel_id=1, source_target_pairs={{0,1},{1,2},{2,3},{3,0},{4,5},{5,6},{6,7},{7,4},{8,9},{9,10},{10,1... | collective-permute-start | bytes 1179656 | tf_op jit(solution)/shard_map/ppermute | solution.py:17
  16.0 10.4 %collective-permute-start.2 = (bf16[768,256]{1,0:T(8,128)(2,1)S(1)}, bf16[768,256]{1,0:T(8,128)(2,1)S(1)}, u32[]{:S(2)}, u32[]{:S(2)}) collective-permute-start(bf16[768,256]{1,0:T(8,128)(2,1)S(1)} %collective-permute-done.1), channel_id=1, source_target_pairs={{0,1},{1,2},{2,3},{3,0},{4,5},{5,6},{6,7},{7,4},{8,9},{9,10},{10,1... | collective-permute-start | bytes 1179656 | tf_op jit(solution)/shard_map/ppermute | solution.py:17
  26.5 0.8 copy-start.1
  27.3 67.6 %copy-start.2 = (s32[768]{0:T(1024)S(1)}, s32[768]{0:T(1024)}, u32[]{:S(2)}) copy-start(s32[768]{0:T(1024)} %param.14) | copy-start | bytes 9220
